TPU v7x, 32 devices: a whole 2x2x4 slice. The times are simulated.
32 devices in a mesh: row: 4 (over x, core), theta: 4 (over z), phi: 2 (over y).
Axes of the slice: x: 2, y: 2, z: 4, core: 2. Of those that a mesh axis runs over, the one named last changes fastest.
Arguments:
- magnetic: float32 [3, 48, 64, 256], P(None, 'row', 'theta', 'phi'), may hold values from -6 to 6
- electric: float32 [3, 48, 64, 256], P(None, 'row', 'theta', 'phi'), may hold values from -6 to 6
Outputs:
- magnetic_new: float32 [3, 48, 64, 256], P(None, 'row', 'theta', 'phi')
- electric_new: float32 [3, 48, 64, 256], P(None, 'row', 'theta', 'phi')
All inputs are finite; a program needn't handle non-finite values.
Results may differ from a plain program's by a relative error of at most 0.0001.
Values sent between devices are 32-bit elements; how exact they have to be, the bound alone decides.
A program may use at most 64 MiB of HBM per device.

v0:
```python
import functools
import math

import jax
import jax.numpy as jnp
from jax import lax
from jax.experimental import pallas as pl
from jax.experimental.pallas import tpu as pltpu
from jax.sharding import PartitionSpec as P

MESH = pl.DeviceIdType.MESH
hole_mass = 1.0
inner_radius = 1.8
wave_speed = 1.25
courant = 0.3
smooth_eps = 1e-06
G = 3
ZERO = ((0, 3), (1, 4), (2, 5))


def flux_of(dim, u, a, s):
    b1, b2, b3, d1, d2, d3 = u
    if dim == 0:
        e2, e3 = a * d2 - s * b3, a * d3 + s * b2
        h2, h3 = a * b2 + s * d3, a * b3 - s * d2
        return [None, -e3, e2, None, h3, -h2]
    if dim == 1:
        e1, e3 = a * d1, a * d3 + s * b2
        h1, h3 = a * b1, a * b3 - s * d2
        return [e3, None, -e1, -h3, None, h1]
    e1, e2 = a * d1, a * d2 - s * b3
    h1, h2 = a * b1, a * b2 + s * d3
    return [-e2, e1, None, h2, -h1, None]


def split(dim, u, a, s):
    out = []
    for f, x in zip(flux_of(dim, u, a, s), u):
        k = wave_speed * x
        out.append((k, -k) if f is None else (f + k, f - k))
    return out


class Line:
    def __init__(self, d, r=None, t3=None):
        self.made, self.d0, self.r0, self.t0 = {}, d, r, t3

    def keep(self, kind, i, make):
        if (kind, i) not in self.made:
            self.made[kind, i] = make()
        return self.made[kind, i]

    def d(self, i):
        return self.keep(0, i, lambda: self.d0(i))

    def square(self, i):
        k, eps = 0.609375, 3.0 * smooth_eps
        return (k * self.d(i)) * self.d(i) + eps

    def r(self, i):
        return self.keep(1, i, lambda: self.r0(i) if self.r0 else self.square(i))

    def q(self, i):
        return self.keep(2, i, lambda: 1.375 * self.d(i))

    def h(self, i):
        return self.keep(3, i, lambda: 0.625 * self.d(i))

    def step(self, i):
        return self.keep(4, i, lambda: self.d(i) - self.d(i - 1))

    def third(self, i):
        return self.step(i + 1) - self.step(i)

    def t(self, i):
        return self.keep(5, i, lambda: self.t0(i) if self.t0 else self.third(i))


def correction(line, i, way):
    i0, i1, i3 = i - 2 * way, i - way, i + way
    x0 = line.d(i0) - line.q(i1)
    x1 = line.d(i1) - line.h(i)
    x2 = line.d(i3) - line.q(i)
    s0, s1, s2 = x0 * x0 + line.r(i1), x1 * x1 + line.r(i), x2 * x2 + line.r(i)
    s0, s1, s2 = s0 * s0, s1 * s1, s2 * s2
    z = 3.0 * s0
    n0, n2, y = s1 * s2, z * s1, z * s2
    den = (n0 + n2) + (y + y)
    return ((n0 + n0) * line.t(i1) + n2 * line.t(i)) * pl.reciprocal(den, approx=True)


def face(p, m, double, i=0):
    if m is None:
        return p.t(i) - (correction(p, i, 1) + correction(p, i, -1))
    dm = m.d(i)
    lin = 6.0 * double + ((p.d(i - 1) - m.d(i + 1)) + 2.0 * (p.d(i) + (dm + dm)))
    return lin - (correction(p, i, 1) - correction(m, i, -1))


def line_of(values, start=0):
    return Line(lambda i: values[i + 1 - start] - values[i - start])


def kernel(sizes, mag, ele, mag_out, ele_out, u, pa, pb, sa, sb, ra, rb, te, tr, fr, acc, vr, vt, vd, vs, gb, pd,
           ca, cs, crp, crm, cth, send, recv, local):
    n_row, n_theta, n_phi, nr, nt, L, plane = sizes
    row, th, ph = lax.axis_index("row"), lax.axis_index("theta"), lax.axis_index("phi")
    slot = L // nr
    halves = nt // 8
    spacing = math.pi / (nt * n_theta)
    spacing_phi = 2.0 * math.pi / (L * n_phi)
    dt = courant / (1.0 / spacing + 1.0 / spacing + 1.0 / spacing_phi)
    scale = -dt / 12.0
    planes = nr + 2 * G
    flat = u.reshape(u.shape[0], 6, (planes + 2) * plane, L)
    first, last = th == 0, th == n_theta - 1
    opposite = (row, th, lax.rem(ph + n_phi // 2, n_phi))
    right = (row, th, lax.rem(ph + 1, n_phi))
    left = (row, th, lax.rem(ph + n_phi - 1, n_phi))
    above = tuple(jnp.where(last, o, q) for o, q in zip(opposite, (row, th + 1, ph)))
    below = tuple(jnp.where(first, o, q) for o, q in zip(opposite, (row, th - 1, ph)))
    outer, inner = (row + 1, th, ph), (row - 1, th, ph)
    has_outer, has_inner = row < n_row - 1, row > 0

    loads = [
        pltpu.make_async_copy(src, u.at[0, 3 * i : 3 * i + 3, 1 + G : 1 + G + nr, 0:nt], local.at[i])
        for i, src in enumerate((mag, ele))
    ]
    for c in loads:
        c.start()

    barrier = pltpu.get_barrier_semaphore()
    for target in (above, below, right, left):
        pl.semaphore_signal(barrier, inc=1, device_id=target, device_id_type=MESH)

    @pl.when(has_outer)
    def _():
        pl.semaphore_signal(barrier, inc=1, device_id=outer, device_id_type=MESH)

    @pl.when(has_inner)
    def _():
        pl.semaphore_signal(barrier, inc=1, device_id=inner, device_id_type=MESH)

    lane = lax.broadcasted_iota(jnp.int32, (8, L), 1)
    sub = lax.broadcasted_iota(jnp.int32, (8, L), 0)
    owner = jnp.zeros((8, L), jnp.int32)
    for q in range(1, nr):
        owner = owner + (lane >= slot * q).astype(jnp.int32)
    in_slot = lane - slot * owner

    def radius_at(index):
        return inner_radius + (index.astype(jnp.float32) + 0.5) * spacing

    def lapse_shift(radius):
        ratio = 2.0 * hole_mass / radius
        return 1.0 / jnp.sqrt(1.0 + ratio), ratio / (1.0 + ratio)

    for q in range(ca.shape[0] // 8):
        a, s = lapse_shift(radius_at(row * nr - G + 8 * q + sub))
        ca[8 * q : 8 * q + 8] = a
        cs[8 * q : 8 * q + 8] = s
    for q in range(crp.shape[0] // 8):
        index = row * nr + 8 * q + sub
        rc, hi, lo = radius_at(index), radius_at(index + 1), radius_at(index - 1)
        crp[8 * q : 8 * q + 8] = scale * (0.5 * (rc + hi)) ** 2 / (rc * rc * spacing)
        crm[8 * q : 8 * q + 8] = scale * (0.5 * (rc + lo)) ** 2 / (rc * rc * spacing)
    for q in range(halves):
        index = (th * nt + 8 * q + sub).astype(jnp.float32)
        mid = jnp.sin((index + 0.5) * spacing)
        cth[0, 8 * q : 8 * q + 8] = scale * jnp.sin((index + 1.0) * spacing) / (mid * spacing)
        cth[1, 8 * q : 8 * q + 8] = scale * jnp.sin(index * spacing) / (mid * spacing)
    a_lane, s_lane = lapse_shift(radius_at(row * nr + owner))
    coef_phi = scale / spacing_phi

    zeros = jnp.zeros((nt, L), jnp.float32)
    for stage in range(3):
        @pl.when(row == 0)
        def _():
            for c in range(6):
                for q in range(G):
                    u[stage, c, 1 + q, 0:nt] = zeros

        @pl.when(row == n_row - 1)
        def _():
            for c in range(6):
                for q in range(G):
                    u[stage, c, 1 + G + nr + q, 0:nt] = zeros

    def pack(stage, r, tiles):
        mask = (lane >= slot * r) & (lane < slot * r + slot)
        for c in range(6):
            for t in range(halves):
                x = tiles[c][t]
                pa[stage, c, t] = jnp.where(mask, pltpu.roll(x, slot * r + 3, 1), pa[stage, c, t])
                pb[stage, c, t] = jnp.where(
                    mask, pltpu.roll(x, lax.rem(slot * r + 6, L), 1), pb[stage, c, t]
                )

    def tile(stage, c, r, t):
        return u[stage, c, 1 + G + r, 8 * t : 8 * t + 8]

    def remote(src, dst, stage, m_send, m_recv, target):
        return pltpu.make_async_remote_copy(
            src_ref=src, dst_ref=dst, send_sem=send.at[stage, m_send], recv_sem=recv.at[stage, m_recv],
            device_id=target, device_id_type=MESH,
        )

    base = 1 + G

    def radial_out(stage):
        return remote(u.at[stage, :, base + nr - G : base + nr, 0:nt], u.at[stage, :, 1 : 1 + G, 0:nt],
                      stage, 0, 0, outer)

    def radial_in(stage):
        return remote(u.at[stage, :, base : base + G, 0:nt],
                      u.at[stage, :, base + nr : base + nr + G, 0:nt], stage, 1, 1, inner)

    def theta_copies(stage):
        up = jnp.where(last, 1, 0)
        down = jnp.where(first, 0, 1)
        return (
            remote(te.at[stage, 1], tr.at[stage, up], stage, 2, 2 + up, above),
            remote(te.at[stage, 0], tr.at[stage, down], stage, 3, 2 + down, below),
        )

    def phi_copies(stage):
        return (
            remote(sa.at[stage], ra.at[stage], stage, 4, 4, right),
            remote(sb.at[stage], rb.at[stage], stage, 5, 5, left),
        )

    starts = list(range(0, nr - 7, 8))
    if starts[-1] + 8 < nr:
        starts.append(nr - 8)

    def grab(stage, c, r0, k):
        return flat[stage, c, pl.ds((base + r0) * plane + k, 8, stride=plane), :]

    def send_all(stage):
        @pl.when(has_outer)
        def _():
            radial_out(stage).start()

        @pl.when(has_inner)
        def _():
            radial_in(stage).start()

        for g in range(2):
            for t in range(halves):
                x, y = pa[stage, 3 * g + 1, t], pa[stage, 3 * g + 2, t]
                x = jnp.where(in_slot < 6, pltpu.roll(x, 3, 1), pltpu.roll(y, 6, 1))
                sa[stage, g, t] = jnp.where(in_slot < 3, pa[stage, 3 * g, t], x)
                x, y = pb[stage, 3 * g + 1, t], pb[stage, 3 * g + 2, t]
                x = jnp.where(in_slot < 3, pltpu.roll(y, L - 6, 1), pltpu.roll(x, L - 3, 1))
                sb[stage, g, t] = jnp.where(in_slot < 6, x, pb[stage, 3 * g, t])
        for side in range(2):
            for c in range(6):
                for k in range(G):
                    for r0 in starts:
                        te[stage, side, pl.ds((c * G + k) * nr + r0, 8), :] = grab(
                            stage, c, r0, k if side == 0 else nt - G + k
                        )
        for c in theta_copies(stage) + phi_copies(stage):
            c.start()

    for c in loads:
        c.wait()

    def pack_first(r, carry):
        pack(0, r, [[tile(0, c, r, t) for t in range(halves)] for c in range(6)])
        return carry

    lax.fori_loop(0, nr, pack_first, 0)
    pl.semaphore_wait(barrier, 4 + jnp.where(has_outer, 1, 0) + jnp.where(has_inner, 1, 0))
    send_all(0)

    def rolled(v, k):
        return v if k == 0 else pltpu.roll(v, (-k) % L, 1)

    def turning(v):
        made = {}

        def at(kind, i, make):
            if i == 0:
                if kind not in made:
                    made[kind] = make()
                return made[kind]
            return rolled(at(kind, 0, make), i)

        line = Line(
            lambda i: at(0, i, lambda: rolled(v, 1) - v),
            lambda i: at(1, i, lambda: line.square(0)),
            lambda i: at(2, i, lambda: line.third(0)),
        )
        return line

    def phi_div(split_values):
        out = []
        for c, (vp, vm) in enumerate(split_values):
            f = face(turning(vp), None if c in ZERO[2] else turning(vm), vp + vm)
            out.append(coef_phi * (f - pltpu.roll(f, 1, 1)))
        return out

    def coefs(p):
        return (
            jnp.broadcast_to(ca[pl.ds(p, 1), :], (8, L)),
            jnp.broadcast_to(cs[pl.ds(p, 1), :], (8, L)),
        )

    def stage_body(stage, carry):
        def phi_pass(r, carry):
            a, s = coefs(r + G)
            for t in range(halves):
                x = [tile(stage, c, r, t) for c in range(6)]
                for c, d in enumerate(phi_div(split(2, x, a, s))):
                    acc[c, r, 8 * t : 8 * t + 8] = d
                for c, (vp, vm) in enumerate(split(0, x, a, s)):
                    vr[0, c, r + G, 8 * t : 8 * t + 8] = vp
                    vr[1, c, r + G, 8 * t : 8 * t + 8] = vm
            return carry

        lax.fori_loop(0, nr, phi_pass, 0)

        def radial_faces(lo, hi):
            def part(t, carry):
                rows = pl.ds(pl.multiple_of(8 * t, 8), 8)
                for c in range(6):
                    p = [vr[0, c, k, rows] for k in range(lo, hi + 5)]
                    pline, mline, m = line_of(p, lo), None, None
                    if c not in ZERO[0]:
                        m = [vr[1, c, k, rows] for k in range(lo, hi + 5)]
                        mline = line_of(m, lo)
                    for f in range(lo, hi):
                        i = f + 2
                        double = None if m is None else p[i - lo] + m[i - lo]
                        fr[c, f, rows] = face(pline, mline, double, i)
                return carry

            lax.fori_loop(0, halves, part, 0)

        radial_faces(G, nr - G + 1)

        @pl.when(has_inner)
        def _():
            radial_out(stage).wait_recv()

        @pl.when(has_outer)
        def _():
            radial_in(stage).wait_recv()

        def ghost_planes(q, carry):
            p = jnp.where(q < G, q, q + nr)
            a, s = coefs(p)
            for t in range(halves):
                x = [u[stage, c, 1 + p, 8 * t : 8 * t + 8] for c in range(6)]
                for c, (vp, vm) in enumerate(split(0, x, a, s)):
                    vr[0, c, p, 8 * t : 8 * t + 8] = vp
                    vr[1, c, p, 8 * t : 8 * t + 8] = vm
            return carry

        lax.fori_loop(0, 2 * G, ghost_planes, 0)

        radial_faces(0, G)
        radial_faces(nr - G + 1, nr + 1)

        for side in range(2):
            remote(te.at[stage, side], tr.at[stage, side], stage, 2, 2 + side, above).wait_recv()
            pole = first if side == 0 else last
            sign = jnp.where(pole, -1.0, 1.0)
            for g in range(G):
                k = jnp.where(pole, G - 1 - g, g)
                for c in range(6):
                    for r0 in starts:
                        x = tr[stage, side, pl.ds((c * G + k) * nr + r0, 8), :]
                        if c % 3:
                            x = x * sign
                        target = (base + r0) * plane + (g - G if side == 0 else nt + g)
                        flat[stage, c, pl.ds(target, 8, stride=plane), :] = x

        for r0 in starts:
            a, s = ca[G + r0 : G + r0 + 8], cs[G + r0 : G + r0 + 8]
            v = [split(1, [grab(stage, c, r0, k) for c in range(6)], a, s) for k in range(-3, 3)]
            for c in range(6):
                pline = line_of([v[k][c][0] for k in range(6)], -2)
                mline = None if c in ZERO[1] else line_of([v[k][c][1] for k in range(6)], -2)
                gb[c, r0 : r0 + 8] = face(pline, mline, v[2][c][0] + v[2][c][1])

        for c in phi_copies(stage):
            c.wait_recv()

        def packed(t, carry):
            xa = [
                jnp.where(in_slot < 3, rolled(ra[stage, c // 3, t], 3 * (c % 3)), pa[stage, c, t])
                for c in range(6)
            ]
            xb = [
                jnp.where(in_slot >= 6, rolled(rb[stage, c // 3, t], -3 * (c % 3)), pb[stage, c, t])
                for c in range(6)
            ]
            da = phi_div(split(2, xa, a_lane, s_lane))
            db = phi_div(split(2, xb, a_lane, s_lane))
            for c in range(6):
                pd[c, t] = jnp.where(in_slot < 6, db[c], pltpu.roll(da[c], 3, 1))
            return carry

        lax.fori_loop(0, halves, packed, 0)

        w = jnp.where(stage == 0, 0.0, jnp.where(stage == 1, 0.75, 1.0 / 3.0)).astype(jnp.float32)
        edge = (lane < 3) | (lane >= L - 3)

        def final(r, carry):
            a, s = coefs(r + G)
            top = (base + r) * plane - G
            for q in range(halves + 1):
                x = [flat[stage, c, pl.ds(top + 8 * q, 8), :] for c in range(6)]
                for c, values in enumerate(split(1, x, a, s)):
                    for sign, v in enumerate(values):
                        vt[sign, c, 8 * q : 8 * q + 8] = v
            for c in range(6):
                for sign in range(1 if c in ZERO[1] else 2):
                    for q in range(halves + 1):
                        d = vt[sign, c, 8 * q + 1 : 8 * q + 9] - vt[sign, c, 8 * q : 8 * q + 8]
                        vd[sign, c, 8 * q : 8 * q + 8] = d
                        vs[sign, c, 8 * q : 8 * q + 8] = Line(lambda i: d).square(0)
            rp = jnp.broadcast_to(crp[pl.ds(r, 1), :], (8, L))
            rm = jnp.broadcast_to(crm[pl.ds(r, 1), :], (8, L))
            new = [[None] * halves for _ in range(6)]
            for c in range(6):
                before = jnp.broadcast_to(gb[c, pl.ds(r, 1), :], (8, L))
                for t in range(halves):
                    rows = slice(8 * t, 8 * t + 8)
                    lines = [
                        Line(lambda i, g=g: vd[g, c, 8 * t + 3 + i : 8 * t + 11 + i],
                             lambda i, g=g: vs[g, c, 8 * t + 3 + i : 8 * t + 11 + i])
                        for g in range(1 if c in ZERO[1] else 2)
                    ]
                    here = slice(8 * t + 3, 8 * t + 11)
                    double = None if c in ZERO[1] else vt[0, c, here] + vt[1, c, here]
                    f = face(lines[0], lines[1] if len(lines) > 1 else None, double)
                    turned = pltpu.roll(f, 1, 0)
                    lower = jnp.where(sub == 0, before, turned)
                    before = turned
                    patch = pltpu.roll(pd[c, t], lax.rem(L + L - 6 - slot * r, L), 1)
                    rate = jnp.where(edge, patch, acc[c, r, rows])
                    rate = rate + (cth[0, rows] * f - cth[1, rows] * lower)
                    rate = rate + (rp * fr[c, r + 1, rows] - rm * fr[c, r, rows])
                    new[c][t] = w * tile(0, c, r, t) + (1.0 - w) * (tile(stage, c, r, t) + rate)
            for t in range(halves):
                b, d = [new[c][t] for c in range(3)], [new[c][t] for c in range(3, 6)]
                b2 = jnp.maximum(b[0] * b[0] + b[1] * b[1] + b[2] * b[2], 1.0)
                along = (b[0] * d[0] + b[1] * d[1] + b[2] * d[2]) / b2
                d = [y - along * x for x, y in zip(b, d)]
                d2 = d[0] * d[0] + d[1] * d[1] + d[2] * d[2]
                shrink = jnp.sqrt(b2 / jnp.maximum(d2, b2))
                for c in range(3):
                    new[3 + c][t] = d[c] * shrink
                for c in range(6):
                    u[stage + 1, c, base + r, 8 * t : 8 * t + 8] = new[c][t]

            @pl.when(stage < 2)
            def _():
                pack(stage + 1, r, new)

            return carry

        lax.fori_loop(0, nr, final, 0)

        @pl.when(stage < 2)
        def _():
            send_all(stage + 1)

        return carry

    lax.fori_loop(0, 3, stage_body, 0)
    stores = [
        pltpu.make_async_copy(u.at[3, 3 * i : 3 * i + 3, base : base + nr, 0:nt], dst, local.at[i])
        for i, dst in enumerate((mag_out, ele_out))
    ]
    for c in stores:
        c.start()

    def drain(stage, carry):
        @pl.when(has_outer)
        def _():
            radial_out(stage).wait_send()

        @pl.when(has_inner)
        def _():
            radial_in(stage).wait_send()

        for c in theta_copies(stage) + phi_copies(stage):
            c.wait_send()
        return carry

    lax.fori_loop(0, 3, drain, 0)
    for c in stores:
        c.wait()


def solution(mesh):
    n_row, n_theta, n_phi = (mesh.shape[k] for k in ("row", "theta", "phi"))

    def body(magnetic, electric):
        _, nr, nt, lanes = magnetic.shape
        plane = -(-(nt + 2 * G) // 8) * 8
        planes = nr + 2 * G
        halves = nt // 8
        pad8 = lambda n: -(-n // 8) * 8
        f32 = jnp.float32
        vm = lambda *shape: pltpu.VMEM(shape, f32)
        sizes = (n_row, n_theta, n_phi, nr, nt, lanes, plane)
        anywhere = pl.BlockSpec(memory_space=pl.ANY)
        packs = vm(3, 6, halves, 8, lanes)
        joined = vm(3, 2, halves, 8, lanes)
        return pl.pallas_call(
            functools.partial(kernel, sizes),
            out_shape=[jax.ShapeDtypeStruct(magnetic.shape, f32)] * 2,
            in_specs=[anywhere] * 2,
            out_specs=[anywhere] * 2,
            scratch_shapes=[
                vm(4, 6, planes + 2, plane, lanes),
                packs, packs,
                joined, joined, joined, joined,
                vm(3, 2, 6 * G * nr, lanes),
                vm(3, 2, 6 * G * nr, lanes),
                vm(6, nr + 1, nt, lanes),
                vm(6, nr, nt, lanes),
                vm(2, 6, planes, nt, lanes),
                vm(2, 6, nt + 16, lanes),
                vm(2, 6, nt + 16, lanes),
                vm(2, 6, nt + 16, lanes),
                vm(6, pad8(nr), lanes),
                vm(6, halves, 8, lanes),
                vm(pad8(planes), lanes),
                vm(pad8(planes), lanes),
                vm(pad8(nr), lanes),
                vm(pad8(nr), lanes),
                vm(2, nt, lanes),
                pltpu.SemaphoreType.DMA((3, 6)),
                pltpu.SemaphoreType.DMA((3, 6)),
                pltpu.SemaphoreType.DMA((2,)),
            ],
            compiler_params=pltpu.CompilerParams(
                collective_id=0, has_side_effects=True
            ),
        )(magnetic, electric)

    spec = P(None, "row", "theta", "phi")
    return jax.shard_map(body, mesh=mesh, in_specs=(spec, spec), out_specs=(spec, spec), check_vma=False)
```

profile of v0, /device:TPU:0, one launch (start us, length us, event | category | flops | bytes accessed | tf_op | source)
XLA Modules:
  0.0 39.4 jit_solution(8025030144503415337)
XLA Ops:
  0.6 36.3 %shard_map.41 = (f32[3,12,16,128]{3,2,1,0:T(8,128)}, f32[3,12,16,128]{3,2,1,0:T(8,128)}) custom-call(f32[3,12,16,128]{3,2,1,0:T(8,128)} %mag.1, f32[3,12,16,128]{3,2,1,0:T(8,128)} %ele.1), custom_call_target="tpu_custom_call" | custom-call | tf_op jit(solution)/shard_map/pallas_call | solution.py:515
  36.9 0.0 copy-start
  36.9 1.7 %copy.6 = f32[3,12,16,128]{3,2,1,0:T(8,128)} copy(f32[3,12,16,128]{3,2,1,0:T(8,128)} %get-tuple-element.4) | data formatting | bytes 589824
  38.7 0.0 copy-done
  38.7 0.7 %copy.7 = f32[3,12,16,128]{3,2,1,0:T(8,128)} copy(f32[3,12,16,128]{3,2,1,0:T(8,128)S(1)} %copy-done) | data formatting | bytes 589824
Async XLA Ops:
  36.9 1.8 %copy-start = (f32[3,12,16,128]{3,2,1,0:T(8,128)S(1)}, f32[3,12,16,128]{3,2,1,0:T(8,128)}, u32[]{:S(2)}) copy-start(f32[3,12,16,128]{3,2,1,0:T(8,128)} %get-tuple-element.5) | copy-start | bytes 884740
where the time goes:
time: 39.6 us; the launch traced here: 39.4 us
  Pallas kernels  36.3 us (92%)
  local copies, waits for them, and re-layouts  2.46 us (6%)
  between operations  0.65 us (2%)
    pallas_call x1, Pallas kernels, body(): pl.pallas_call(functools.partial(kernel, sizes), out_shape=[jax.ShapeDtyp...  36.3 us
    unnamed x4, local copies, waits for them, and re-layouts  2.46 us

commit v1 on v0

v1 whole, which is shorter than its diff:
```python
import functools
import math

import jax
import jax.numpy as jnp
from jax import lax
from jax.experimental import pallas as pl
from jax.experimental.pallas import tpu as pltpu
from jax.sharding import PartitionSpec as P

MESH = pl.DeviceIdType.MESH
hole_mass = 1.0
inner_radius = 1.8
wave_speed = 1.25
courant = 0.3
smooth_eps = 1e-06
G = 3

AXES = ((1, 2, 4, 5, 0, 3), (0, 2, 3, 5, 1, 4))
PAD = 1


def kept(make):
    made = {}

    def get(i):
        if i not in made:
            made[i] = make(i)
        return made[i]

    return get


class Line:
    def __init__(self, v):
        self.v = v
        self.d = kept(lambda i: v(i + 1) - v(i))
        self.e = kept(lambda i: self.d(i) * self.d(i))
        self.ee = kept(lambda i: self.e(i) + 3.0 * smooth_eps)
        self.f = kept(lambda i: 2.5 * self.e(i))
        self.p = kept(lambda i: self.d(i - 1) * self.d(i))
        self.b = kept(lambda i: 2.75 * self.p(i))
        self.step = kept(lambda i: self.d(i) - self.d(i - 1))
        self.t = kept(lambda i: self.step(i + 1) - self.step(i))
        self.tt = kept(lambda i: self.t(i) + self.t(i))
        self.low = kept(lambda i: self.weight((self.ee(i - 1) + self.f(i)) - self.b(i)))
        self.mid = kept(lambda i: 6.0 * self.weight((self.ee(i - 1) + self.e(i)) - 1.25 * self.p(i)))
        self.high = kept(lambda i: self.weight((self.ee(i) + self.f(i - 1)) - self.b(i)))

    def weight(self, smooth):
        q = pl.reciprocal(smooth, approx=True)
        return q * q

    def up(self, c):
        return self.blend(self.low(c - 1), self.mid(c), 3.0 * self.high(c + 1), self.tt(c - 1), self.t(c))

    def down(self, c):
        return self.blend(self.high(c + 2), self.mid(c + 1), 3.0 * self.low(c), self.tt(c + 1), self.t(c))

    def blend(self, w0, w1, w2, t0, t2):
        den = (w0 + w2) + w1
        return (w0 * t0 + w2 * t2) * pl.reciprocal(den, approx=True)


def faces(k, f, which):
    k = kept(k)
    if f is None:
        line = Line(k)
        for i in which:
            c = i + 2
            yield i, line.t(c) - (line.up(c) + line.down(c))
        return
    f = kept(f)
    plus, minus = Line(kept(lambda i: f(i) + k(i))), Line(kept(lambda i: f(i) - k(i)))
    f10, f4, f2 = (kept(lambda i, x=x: x * f(i)) for x in (10.0, 4.0, 2.0))
    for i in which:
        c = i + 2
        lin = ((f10(c) + f4(c + 1)) - f2(c - 1)) - minus.t(c)
        yield i, lin - (plus.up(c) - minus.down(c))


def kernel(sizes, mag, ele, mag_out, ele_out, u, te, tr, pe, pr, tt, dd, kr, fr, kt, ft, gr, gt, acc,
           ca, cs, car, csr, crp, crm, cth, lane_a, lane_s, send, recv, local):
    n_row, n_theta, n_phi, nr, nt, L = sizes
    row, th, ph = lax.axis_index("row"), lax.axis_index("theta"), lax.axis_index("phi")
    halves = nt // 8
    spacing = math.pi / (nt * n_theta)
    spacing_phi = 2.0 * math.pi / (L * n_phi)
    dt = courant / (1.0 / spacing + 1.0 / spacing + 1.0 / spacing_phi)
    scale = -dt / 12.0
    coef_phi = scale / spacing_phi
    planes = nr + 2 * G
    rows6, rows4 = 6 * nr, 4 * nr
    full, rest = L // nt, nr - L // nt
    seg = L // 8
    jump = seg + PAD
    first_row = 16
    blocks = pe.shape[3]
    te_rows = te.reshape(3, 2, 8 * rows6, L)
    pe_rows = pe.reshape(3, 2, 8 * blocks, L)
    pr_rows = pr.reshape(3, 2, 8 * blocks, L)

    def place(m):
        return m % seg + (m // seg) * jump

    first, last = th == 0, th == n_theta - 1
    opposite = (row, th, lax.rem(ph + n_phi // 2, n_phi))
    right = (row, th, lax.rem(ph + 1, n_phi))
    left = (row, th, lax.rem(ph + n_phi - 1, n_phi))
    above = tuple(jnp.where(last, o, q) for o, q in zip(opposite, (row, th + 1, ph)))
    below = tuple(jnp.where(first, o, q) for o, q in zip(opposite, (row, th - 1, ph)))
    outer, inner = (row + 1, th, ph), (row - 1, th, ph)
    has_outer, has_inner = row < n_row - 1, row > 0

    loads = [
        pltpu.make_async_copy(src, u.at[0, 3 * i : 3 * i + 3, G : G + nr], local.at[i])
        for i, src in enumerate((mag, ele))
    ]
    for c in loads:
        c.start()

    barrier = pltpu.get_barrier_semaphore()
    for target in (above, below, right, left):
        pl.semaphore_signal(barrier, inc=1, device_id=target, device_id_type=MESH)

    @pl.when(has_outer)
    def _():
        pl.semaphore_signal(barrier, inc=1, device_id=outer, device_id_type=MESH)

    @pl.when(has_inner)
    def _():
        pl.semaphore_signal(barrier, inc=1, device_id=inner, device_id_type=MESH)

    lane = lax.broadcasted_iota(jnp.int32, (8, L), 1)
    sub = lax.broadcasted_iota(jnp.int32, (8, L), 0)

    def radius_at(index):
        return inner_radius + (index.astype(jnp.float32) + 0.5) * spacing

    def lapse_shift(radius):
        ratio = 2.0 * hole_mass / radius
        return 1.0 / jnp.sqrt(1.0 + ratio), ratio / (1.0 + ratio)

    for r0 in (0, nr - 8):
        a, s = lapse_shift(radius_at(row * nr + r0 + sub))
        car[r0 : r0 + 8] = a
        csr[r0 : r0 + 8] = s

    def tables(q, carry):
        index = jnp.full((8, L), row * nr - G + q, jnp.int32)
        a, s = lapse_shift(radius_at(index))
        ca[q] = a
        cs[q] = s
        rc, hi, lo = radius_at(index), radius_at(index + 1), radius_at(index - 1)
        area = scale / (rc * rc * spacing)
        crp[q] = (0.5 * (rc + hi)) ** 2 * area
        crm[q] = (0.5 * (rc + lo)) ** 2 * area
        return carry

    lax.fori_loop(0, planes, tables, 0)
    for q in range(halves):
        index = (th * nt + 8 * q + sub).astype(jnp.float32)
        mid = jnp.sin((index + 0.5) * spacing)
        cth[0, 8 * q : 8 * q + 8] = scale * jnp.sin((index + 1.0) * spacing) / (mid * spacing)
        cth[1, 8 * q : 8 * q + 8] = scale * jnp.sin(index * spacing) / (mid * spacing)

    def owner(x, size):
        out = jnp.zeros((8, L), jnp.int32)
        for q in range(1, L // size):
            out = out + (x >= size * q).astype(jnp.int32)
        return out

    a, s = lapse_shift(radius_at(row * nr + owner(lane, nt)))
    lane_a[0], lane_a[1] = a, -a
    lane_s[0], lane_s[1] = s, s
    second = lane >= L // 2
    a, s = lapse_shift(radius_at(row * nr + full + owner(jnp.where(second, lane - L // 2, lane), nt)))
    lane_a[2], lane_s[2] = jnp.where(second, -a, a), s

    zeros = jnp.zeros((nt, L), jnp.float32)
    for stage in range(3):
        @pl.when(row == 0)
        def _():
            for c in range(6):
                for q in range(G):
                    u[stage, c, q] = zeros

        @pl.when(row == n_row - 1)
        def _():
            for c in range(6):
                for q in range(G):
                    u[stage, c, G + nr + q] = zeros

    def radial_flux(x, a, s):
        b2, b3, d2, d3 = x[1], x[2], x[4], x[5]
        return [-(a * d3 + s * b2), a * d2 - s * b3, a * b3 - s * d2, -(a * b2 + s * d3)]

    def polar_flux(x, a, s):
        b1, b2, b3, d1, d2, d3 = x
        return [a * d3 + s * b2, -(a * d1), s * d2 - a * b3, a * b1]

    def prepare(stage, r, tiles):
        a, s = ca[r + G], cs[r + G]
        for t in range(halves):
            rows = slice(8 * t, 8 * t + 8)
            x = [tiles[c][t] for c in range(6)]
            k = [wave_speed * y for y in x]
            for l, y in enumerate(radial_flux(x, a, s)):
                fr[l, r + G, rows] = y
            for l, c in enumerate(AXES[0]):
                kr[l, r + G, rows] = k[c]
            for l, y in enumerate(polar_flux(x, a, s)):
                ft[pl.ds((G + 8 * t) * rows4 + l * nr + r, 8, stride=rows4), :] = y
            for l, c in enumerate(AXES[1]):
                kt[pl.ds((G + 8 * t) * rows6 + l * nr + r, 8, stride=rows6), :] = k[c]
            for side, edge in enumerate((0, halves - 1)):
                if t == edge:
                    for c in range(6):
                        te_rows[stage, side, pl.ds(c * nr + r, 8, stride=rows6), :] = x[c]

    def turn(stage, out, parts):
        x = [u[stage, c, G + p : G + p + n].reshape(n * nt, L) for c, p, n in parts]
        x = (x[0] if len(x) == 1 else jnp.concatenate(x, axis=0)).T
        for q in range(L // 8):
            tt[out, pl.ds(first_row + place(8 * q), 8), :] = x[8 * q : 8 * q + 8]
        pe_rows[stage, 0, pl.ds(out, 8, stride=blocks), :] = x[0:8]
        pe_rows[stage, 1, pl.ds(out, 8, stride=blocks), :] = x[L - 8 : L]

    def turn_all(stage):
        for c in range(6):
            turn(stage, c, [(c, 0, full)])
        for c in range(3):
            turn(stage, 6 + c, [(c, full, rest), (3 + c, full, rest)])
        for c in range(2):
            turn(stage, 9 + c, [(3 + c, full, rest), (c, full, rest)])

    def remote(src, dst, stage, m_send, m_recv, target):
        return pltpu.make_async_remote_copy(
            src_ref=src, dst_ref=dst, send_sem=send.at[stage, m_send], recv_sem=recv.at[stage, m_recv],
            device_id=target, device_id_type=MESH,
        )

    def radial_out(stage):
        return remote(u.at[stage, :, nr : nr + G], u.at[stage, :, 0:G], stage, 0, 0, outer)

    def radial_in(stage):
        return remote(u.at[stage, :, G : 2 * G], u.at[stage, :, G + nr : nr + 2 * G], stage, 1, 1, inner)

    def theta_copies(stage):
        up = jnp.where(last, 1, 0)
        down = jnp.where(first, 0, 1)
        return (
            remote(te.at[stage, 1, 8 - G : 8], tr.at[stage, up], stage, 2, 2 + up, above),
            remote(te.at[stage, 0, 0:G], tr.at[stage, down], stage, 3, 2 + down, below),
        )

    def phi_copies(stage):
        return (
            remote(pe.at[stage, 1, 8 - G : 8], pr.at[stage, 0, 8 - G : 8], stage, 4, 4, right),
            remote(pe.at[stage, 0, 0:G], pr.at[stage, 1, 0:G], stage, 5, 5, left),
        )

    def send_all(stage):
        @pl.when(has_outer)
        def _():
            radial_out(stage).start()

        @pl.when(has_inner)
        def _():
            radial_in(stage).start()

        for c in theta_copies(stage):
            c.start()
        turn_all(stage)
        for c in phi_copies(stage):
            c.start()

    for c in loads:
        c.wait()

    def prepare_first(r, carry):
        prepare(0, r, [[u[0, c, r + G, 8 * t : 8 * t + 8] for t in range(halves)] for c in range(6)])
        return carry

    lax.fori_loop(0, nr, prepare_first, 0)
    pl.semaphore_wait(barrier, 4 + jnp.where(has_outer, 1, 0) + jnp.where(has_inner, 1, 0))
    send_all(0)

    def radial_faces(which):
        def part(t, carry):
            rows = pl.ds(pl.multiple_of(8 * t, 8), 8)
            for l in range(6):
                k = lambda i: kr[l, i, rows]
                f = (lambda i: fr[l, i, rows]) if l < 4 else None
                for span in which:
                    for i, x in faces(k, f, span):
                        gr[l, i, rows] = x
            return carry

        lax.fori_loop(0, halves, part, 0)

    def polar_faces(which):
        def part(q, carry):
            for j in range(3):
                v = 2 * q + j if j < 2 else 2 * (nr // 4) + q
                k = lambda i: kt[pl.ds(pl.multiple_of(i * rows6 + 8 * v, 8), 8), :]
                f = (lambda i: ft[pl.ds(pl.multiple_of(i * rows4 + 8 * v, 8), 8), :]) if j < 2 else None
                for span in which:
                    for i, x in faces(k, f, span):
                        gt[pl.ds(pl.multiple_of(i * rows6 + 8 * v, 8), 8), :] = x
            return carry

        lax.fori_loop(0, nr // 4, part, 0)

    def azimuth_faces():
        def part(q, carry):
            a, s = lane_a[q], lane_s[q]
            swapped = jnp.where(q == 0, 3, jnp.where(q == 1, 0, 9))

            def at(block, i):
                return tt[block, pl.ds(first_row + place(i - G), 8, stride=jump), :]

            own = [kept(lambda i, c=c: at(3 * q + c, i)) for c in range(3)]
            fluxes = (
                lambda i: s * own[2](i) - a * at(swapped + 1, i),
                lambda i: a * at(swapped, i),
                None,
            )
            for c in range(3):
                before = None
                for i, x in faces(lambda i: wave_speed * own[c](i), fluxes[c], range(seg + 1)):
                    if i:
                        dd[3 * q + c, pl.ds(i - 1, 8, stride=jump), :] = coef_phi * (x - before)
                    before = x
            return carry

        lax.fori_loop(0, 3, part, 0)

    def turn_back():
        for b in range(9):
            x = jnp.concatenate([dd[b, pl.ds(place(8 * q), 8), :] for q in range(L // 8)], axis=0).T
            if b < 6:
                acc[b, 0:full] = x.reshape(full, nt, L)
            else:
                x = x.reshape(2 * rest, nt, L)
                acc[b - 6, full:nr] = x[:rest]
                acc[b - 3, full:nr] = x[rest:]

    inside_r = (range(G, nr - G + 1),)
    edges_r = (range(0, G), range(nr - G + 1, nr + 1))
    inside_t = (range(G, nt - G + 1),)
    edges_t = (range(0, G), range(nt - G + 1, nt + 1))

    def stage_body(stage, carry):
        radial_faces(inside_r)
        polar_faces(inside_t)

        for c in phi_copies(stage):
            c.wait_recv()
        for b in range(11):
            tt[b, pl.ds(first_row + place(-G) - (8 - G), 8), :] = pr_rows[stage, 0, pl.ds(b, 8, stride=blocks), :]
            tt[b, pl.ds(first_row + place(L), 8), :] = pr_rows[stage, 1, pl.ds(b, 8, stride=blocks), :]
        azimuth_faces()
        turn_back()

        @pl.when(has_inner)
        def _():
            radial_out(stage).wait_recv()

        @pl.when(has_outer)
        def _():
            radial_in(stage).wait_recv()

        def ghost_planes(q, carry):
            p = jnp.where(q < G, q, q + nr)
            a, s = ca[p], cs[p]
            for t in range(halves):
                rows = slice(8 * t, 8 * t + 8)
                x = [u[stage, c, p, rows] for c in range(6)]
                for l, y in enumerate(radial_flux(x, a, s)):
                    fr[l, p, rows] = y
                for l, c in enumerate(AXES[0]):
                    kr[l, p, rows] = wave_speed * x[c]
            return carry

        lax.fori_loop(0, 2 * G, ghost_planes, 0)
        radial_faces(edges_r)

        for side in range(2):
            remote(te.at[stage, side, 0:G], tr.at[stage, side], stage, 2, 2 + side, above).wait_recv()
            pole = first if side == 0 else last
            sign = jnp.where(pole, -1.0, 1.0)
            for g in range(G):
                k = jnp.where(pole, G - 1 - g, g)
                target = g if side == 0 else G + nt + g
                for r0 in (0, nr - 8):
                    a, s = car[r0 : r0 + 8], csr[r0 : r0 + 8]
                    x = [tr[stage, side, k, c * nr + r0 : c * nr + r0 + 8] for c in range(6)]
                    x = [y * sign if c % 3 else y for c, y in enumerate(x)]
                    for l, y in enumerate(polar_flux(x, a, s)):
                        ft[pl.ds(target * rows4 + l * nr + r0, 8), :] = y
                    for l, c in enumerate(AXES[1]):
                        kt[pl.ds(target * rows6 + l * nr + r0, 8), :] = wave_speed * x[c]
        polar_faces(edges_t)

        w = jnp.where(stage == 0, 0.0, jnp.where(stage == 1, 0.75, 1.0 / 3.0)).astype(jnp.float32)

        def update(r):
            rp, rm = crp[r + G], crm[r + G]
            new = [[None] * halves for _ in range(6)]
            for t in range(halves):
                rows = slice(8 * t, 8 * t + 8)
                for c in range(6):
                    lr, lt = AXES[0].index(c), AXES[1].index(c)
                    low = gt[pl.ds(8 * t * rows6 + lt * nr + r, 8, stride=rows6), :]
                    high = gt[pl.ds((8 * t + 1) * rows6 + lt * nr + r, 8, stride=rows6), :]
                    rate = acc[c, r, rows] + (cth[0, rows] * high - cth[1, rows] * low)
                    rate = rate + (rp * gr[lr, r + 1, rows] - rm * gr[lr, r, rows])
                    new[c][t] = w * u[0, c, r + G, rows] + (1.0 - w) * (u[stage, c, r + G, rows] + rate)
                b, d = [new[c][t] for c in range(3)], [new[c][t] for c in range(3, 6)]
                b2 = jnp.maximum(b[0] * b[0] + b[1] * b[1] + b[2] * b[2], 1.0)
                along = (b[0] * d[0] + b[1] * d[1] + b[2] * d[2]) * pl.reciprocal(b2, approx=True)
                d = [y - along * x for x, y in zip(b, d)]
                d2 = d[0] * d[0] + d[1] * d[1] + d[2] * d[2]
                shrink = b2 * lax.rsqrt(b2 * jnp.maximum(d2, b2))
                for c in range(3):
                    new[3 + c][t] = d[c] * shrink
                for c in range(6):
                    u[stage + 1, c, r + G, rows] = new[c][t]
            return new

        pair = 2 if nr % 2 == 0 else 1

        def final(i, carry):
            new = [update(pair * i + j) for j in range(pair)]

            @pl.when(stage < 2)
            def _():
                for j in range(pair):
                    prepare(stage + 1, pair * i + j, new[j])

            return carry

        lax.fori_loop(0, nr // pair, final, 0)

        @pl.when(stage < 2)
        def _():
            send_all(stage + 1)

        return carry

    lax.fori_loop(0, 3, stage_body, 0)
    stores = [
        pltpu.make_async_copy(u.at[3, 3 * i : 3 * i + 3, G : G + nr], dst, local.at[i])
        for i, dst in enumerate((mag_out, ele_out))
    ]
    for c in stores:
        c.start()

    def drain(stage, carry):
        @pl.when(has_outer)
        def _():
            radial_out(stage).wait_send()

        @pl.when(has_inner)
        def _():
            radial_in(stage).wait_send()

        for c in theta_copies(stage) + phi_copies(stage):
            c.wait_send()
        return carry

    lax.fori_loop(0, 3, drain, 0)
    for c in stores:
        c.wait()


def solution(mesh):
    n_row, n_theta, n_phi = (mesh.shape[k] for k in ("row", "theta", "phi"))

    def body(magnetic, electric):
        _, nr, nt, lanes = magnetic.shape
        planes = nr + 2 * G
        pad8 = lambda n: -(-n // 8) * 8
        f32 = jnp.float32
        vm = lambda *shape: pltpu.VMEM(shape, f32)
        assert nt % 8 == 0 and nr % 4 == 0 and 2 * nr * nt == 3 * lanes
        long = lanes + 8 * PAD
        sizes = (n_row, n_theta, n_phi, nr, nt, lanes)
        anywhere = pl.BlockSpec(memory_space=pl.ANY)
        return pl.pallas_call(
            functools.partial(kernel, sizes),
            out_shape=[jax.ShapeDtypeStruct(magnetic.shape, f32)] * 2,
            in_specs=[anywhere] * 2,
            out_specs=[anywhere] * 2,
            scratch_shapes=[
                vm(4, 6, planes, nt, lanes),
                vm(3, 2, 8, 6 * nr, lanes),
                vm(3, 2, G, 6 * nr, lanes),
                vm(3, 2, 8, 16, lanes),
                vm(3, 2, 8, 16, lanes),
                vm(11, 16 + pad8(long) + 8, lanes),
                vm(9, pad8(long), lanes),
                vm(6, planes, nt, lanes),
                vm(4, planes, nt, lanes),
                vm((nt + 2 * G) * 6 * nr, lanes),
                vm((nt + 2 * G) * 4 * nr, lanes),
                vm(6, nr + 1, nt, lanes),
                vm((nt + 1) * 6 * nr, lanes),
                vm(6, nr, nt, lanes),
                vm(planes, 8, lanes),
                vm(planes, 8, lanes),
                vm(pad8(nr), lanes),
                vm(pad8(nr), lanes),
                vm(planes, 8, lanes),
                vm(planes, 8, lanes),
                vm(2, nt, lanes),
                vm(3, 8, lanes),
                vm(3, 8, lanes),
                pltpu.SemaphoreType.DMA((3, 6)),
                pltpu.SemaphoreType.DMA((3, 6)),
                pltpu.SemaphoreType.DMA((2,)),
            ],
            compiler_params=pltpu.CompilerParams(
                collective_id=0, has_side_effects=True
            ),
        )(magnetic, electric)

    spec = P(None, "row", "theta", "phi")
    return jax.shard_map(body, mesh=mesh, in_specs=(spec, spec), out_specs=(spec, spec), check_vma=False)
```

time: 39.6 us -> 35.5 us (0.90)
  Pallas kernels: 36.3 us -> 32.2 us
    pallas_call x1, Pallas kernels: 36.3 us -> 32.2 us  [body(): pl.pallas_call(functools.partial(kernel, sizes), out_shape=[jax.ShapeDtyp...]
where the time goes in v1:
time: 35.5 us; the launch traced here: 35.3 us
  Pallas kernels  32.2 us (91%)
  local copies, waits for them, and re-layouts  2.46 us (7%)
  between operations  0.65 us (2%)
    pallas_call x1, Pallas kernels, body(): pl.pallas_call(functools.partial(kernel, sizes), out_shape=[jax.ShapeDtyp...  32.2 us
    unnamed x4, local copies, waits for them, and re-layouts  2.46 us

profile of v1, /device:TPU:0, one launch (start us, length us, event | category | flops | bytes accessed | tf_op | source)
XLA Modules:
  0.0 35.3 jit_solution(8775868602961415328)
XLA Ops:
  0.6 32.2 %shard_map.41 = (f32[3,12,16,128]{3,2,1,0:T(8,128)}, f32[3,12,16,128]{3,2,1,0:T(8,128)}) custom-call(f32[3,12,16,128]{3,2,1,0:T(8,128)} %mag.1, f32[3,12,16,128]{3,2,1,0:T(8,128)} %ele.1), custom_call_target="tpu_custom_call" | custom-call | tf_op jit(solution)/shard_map/pallas_call | solution.py:491
  32.8 0.0 copy-start
  32.8 1.7 %copy.6 = f32[3,12,16,128]{3,2,1,0:T(8,128)} copy(f32[3,12,16,128]{3,2,1,0:T(8,128)} %get-tuple-element.4) | data formatting | bytes 589824
  34.6 0.0 copy-done
  34.6 0.7 %copy.7 = f32[3,12,16,128]{3,2,1,0:T(8,128)} copy(f32[3,12,16,128]{3,2,1,0:T(8,128)S(1)} %copy-done) | data formatting | bytes 589824
Async XLA Ops:
  32.8 1.8 %copy-start = (f32[3,12,16,128]{3,2,1,0:T(8,128)S(1)}, f32[3,12,16,128]{3,2,1,0:T(8,128)}, u32[]{:S(2)}) copy-start(f32[3,12,16,128]{3,2,1,0:T(8,128)} %get-tuple-element.5) | copy-start | bytes 884740

commit v2 on v1

--- a/solution.py
+++ b/solution.py
@@ -79,7 +79,7 @@
         yield i, lin - (plus.up(c) - minus.down(c))
 
 
-def kernel(sizes, mag, ele, mag_out, ele_out, u, te, tr, pe, pr, tt, dd, kr, fr, kt, ft, gr, gt, acc,
+def kernel(sizes, mag, ele, mag_out, ele_out, u, te, tr, pe, pr, tt, dd, kr, fr, kt, ft, gr, gt, ga, acc,
            ca, cs, car, csr, crp, crm, cth, lane_a, lane_s, send, recv, local):
     n_row, n_theta, n_phi, nr, nt, L = sizes
     row, th, ph = lax.axis_index("row"), lax.axis_index("theta"), lax.axis_index("phi")
@@ -91,6 +91,7 @@
     coef_phi = scale / spacing_phi
     planes = nr + 2 * G
     rows6, rows4 = 6 * nr, 4 * nr
+    pitch6, pitch4 = rows6 + PAD, rows4 + PAD
     full, rest = L // nt, nr - L // nt
     seg = L // 8
     jump = seg + PAD
@@ -210,9 +211,9 @@
             for l, c in enumerate(AXES[0]):
                 kr[l, r + G, rows] = k[c]
             for l, y in enumerate(polar_flux(x, a, s)):
-                ft[pl.ds((G + 8 * t) * rows4 + l * nr + r, 8, stride=rows4), :] = y
+                ft[pl.ds((G + 8 * t) * pitch4 + l * nr + r, 8, stride=pitch4), :] = y
             for l, c in enumerate(AXES[1]):
-                kt[pl.ds((G + 8 * t) * rows6 + l * nr + r, 8, stride=rows6), :] = k[c]
+                kt[pl.ds((G + 8 * t) * pitch6 + l * nr + r, 8, stride=pitch6), :] = k[c]
             for side, edge in enumerate((0, halves - 1)):
                 if t == edge:
                     for c in range(6):
@@ -269,10 +270,8 @@
         def _():
             radial_in(stage).start()
 
-        for c in theta_copies(stage):
-            c.start()
         turn_all(stage)
-        for c in phi_copies(stage):
+        for c in phi_copies(stage) + theta_copies(stage):
             c.start()
 
     for c in loads:
@@ -303,16 +302,16 @@
         def part(q, carry):
             for j in range(3):
                 v = 2 * q + j if j < 2 else 2 * (nr // 4) + q
-                k = lambda i: kt[pl.ds(pl.multiple_of(i * rows6 + 8 * v, 8), 8), :]
-                f = (lambda i: ft[pl.ds(pl.multiple_of(i * rows4 + 8 * v, 8), 8), :]) if j < 2 else None
+                k = lambda i: kt[pl.ds(i * pitch6 + 8 * v, 8), :]
+                f = (lambda i: ft[pl.ds(i * pitch4 + 8 * v, 8), :]) if j < 2 else None
                 for span in which:
                     for i, x in faces(k, f, span):
-                        gt[pl.ds(pl.multiple_of(i * rows6 + 8 * v, 8), 8), :] = x
+                        gt[pl.ds(i * pitch6 + 8 * v, 8), :] = x
             return carry
 
         lax.fori_loop(0, nr // 4, part, 0)
 
-    def azimuth_faces():
+    def azimuth_faces(which):
         def part(q, carry):
             a, s = lane_a[q], lane_s[q]
             swapped = jnp.where(q == 0, 3, jnp.where(q == 1, 0, 9))
@@ -327,11 +326,19 @@
                 None,
             )
             for c in range(3):
-                before = None
-                for i, x in faces(lambda i: wave_speed * own[c](i), fluxes[c], range(seg + 1)):
-                    if i:
-                        dd[3 * q + c, pl.ds(i - 1, 8, stride=jump), :] = coef_phi * (x - before)
-                    before = x
+                k = lambda i: wave_speed * own[c](i)
+                for span in which:
+                    before = None
+                    for i, x in faces(k, fluxes[c], span):
+                        if i == G or i == seg - G:
+                            ga[3 * q + c, int(i != G)] = x
+                        if before is None and i == seg - G + 1:
+                            before = ga[3 * q + c, 1]
+                        if before is not None:
+                            dd[3 * q + c, pl.ds(i - 1, 8, stride=jump), :] = coef_phi * (x - before)
+                        before = x
+                    if span[-1] == G - 1:
+                        dd[3 * q + c, pl.ds(G - 1, 8, stride=jump), :] = coef_phi * (ga[3 * q + c, 0] - before)
             return carry
 
         lax.fori_loop(0, 3, part, 0)
@@ -349,18 +356,21 @@
     inside_r = (range(G, nr - G + 1),)
     edges_r = (range(0, G), range(nr - G + 1, nr + 1))
     inside_t = (range(G, nt - G + 1),)
+    inside_a = (range(G, seg - G + 1),)
+    edges_a = (range(0, G), range(seg - G + 1, seg + 1))
     edges_t = (range(0, G), range(nt - G + 1, nt + 1))
 
     def stage_body(stage, carry):
         radial_faces(inside_r)
         polar_faces(inside_t)
+        azimuth_faces(inside_a)
 
         for c in phi_copies(stage):
             c.wait_recv()
         for b in range(11):
             tt[b, pl.ds(first_row + place(-G) - (8 - G), 8), :] = pr_rows[stage, 0, pl.ds(b, 8, stride=blocks), :]
             tt[b, pl.ds(first_row + place(L), 8), :] = pr_rows[stage, 1, pl.ds(b, 8, stride=blocks), :]
-        azimuth_faces()
+        azimuth_faces(edges_a)
         turn_back()
 
         @pl.when(has_inner)
@@ -398,9 +408,9 @@
                     x = [tr[stage, side, k, c * nr + r0 : c * nr + r0 + 8] for c in range(6)]
                     x = [y * sign if c % 3 else y for c, y in enumerate(x)]
                     for l, y in enumerate(polar_flux(x, a, s)):
-                        ft[pl.ds(target * rows4 + l * nr + r0, 8), :] = y
+                        ft[pl.ds(target * pitch4 + l * nr + r0, 8), :] = y
                     for l, c in enumerate(AXES[1]):
-                        kt[pl.ds(target * rows6 + l * nr + r0, 8), :] = wave_speed * x[c]
+                        kt[pl.ds(target * pitch6 + l * nr + r0, 8), :] = wave_speed * x[c]
         polar_faces(edges_t)
 
         w = jnp.where(stage == 0, 0.0, jnp.where(stage == 1, 0.75, 1.0 / 3.0)).astype(jnp.float32)
@@ -412,8 +422,8 @@
                 rows = slice(8 * t, 8 * t + 8)
                 for c in range(6):
                     lr, lt = AXES[0].index(c), AXES[1].index(c)
-                    low = gt[pl.ds(8 * t * rows6 + lt * nr + r, 8, stride=rows6), :]
-                    high = gt[pl.ds((8 * t + 1) * rows6 + lt * nr + r, 8, stride=rows6), :]
+                    low = gt[pl.ds(8 * t * pitch6 + lt * nr + r, 8, stride=pitch6), :]
+                    high = gt[pl.ds((8 * t + 1) * pitch6 + lt * nr + r, 8, stride=pitch6), :]
                     rate = acc[c, r, rows] + (cth[0, rows] * high - cth[1, rows] * low)
                     rate = rate + (rp * gr[lr, r + 1, rows] - rm * gr[lr, r, rows])
                     new[c][t] = w * u[0, c, r + G, rows] + (1.0 - w) * (u[stage, c, r + G, rows] + rate)
@@ -425,8 +435,6 @@
                 shrink = b2 * lax.rsqrt(b2 * jnp.maximum(d2, b2))
                 for c in range(3):
                     new[3 + c][t] = d[c] * shrink
-                for c in range(6):
-                    u[stage + 1, c, r + G, rows] = new[c][t]
             return new
 
         pair = 2 if nr % 2 == 0 else 1
@@ -437,8 +445,19 @@
             @pl.when(stage < 2)
             def _():
                 for j in range(pair):
+                    for c in range(6):
+                        for t in range(halves):
+                            u[stage + 1, c, pair * i + j + G, 8 * t : 8 * t + 8] = new[j][c][t]
                     prepare(stage + 1, pair * i + j, new[j])
 
+            @pl.when(stage == 2)
+            def _():
+                for j in range(pair):
+                    for c in range(3):
+                        for t in range(halves):
+                            mag_out[c, pair * i + j, 8 * t : 8 * t + 8] = new[j][c][t]
+                            ele_out[c, pair * i + j, 8 * t : 8 * t + 8] = new[j][3 + c][t]
+
             return carry
 
         lax.fori_loop(0, nr // pair, final, 0)
@@ -450,13 +469,6 @@
         return carry
 
     lax.fori_loop(0, 3, stage_body, 0)
-    stores = [
-        pltpu.make_async_copy(u.at[3, 3 * i : 3 * i + 3, G : G + nr], dst, local.at[i])
-        for i, dst in enumerate((mag_out, ele_out))
-    ]
-    for c in stores:
-        c.start()
-
     def drain(stage, carry):
         @pl.when(has_outer)
         def _():
@@ -471,12 +483,17 @@
         return carry
 
     lax.fori_loop(0, 3, drain, 0)
-    for c in stores:
-        c.wait()
 
 
 def solution(mesh):
     n_row, n_theta, n_phi = (mesh.shape[k] for k in ("row", "theta", "phi"))
+
+    def put_out(m, e, mo, eo, sem):
+        copies = [pltpu.make_async_copy(x, y, sem.at[i]) for i, (x, y) in enumerate(((m, mo), (e, eo)))]
+        for c in copies:
+            c.start()
+        for c in copies:
+            c.wait()
 
     def body(magnetic, electric):
         _, nr, nt, lanes = magnetic.shape
@@ -488,13 +505,13 @@
         long = lanes + 8 * PAD
         sizes = (n_row, n_theta, n_phi, nr, nt, lanes)
         anywhere = pl.BlockSpec(memory_space=pl.ANY)
-        return pl.pallas_call(
+        out = pl.pallas_call(
             functools.partial(kernel, sizes),
-            out_shape=[jax.ShapeDtypeStruct(magnetic.shape, f32)] * 2,
+            out_shape=[pltpu.VMEM(magnetic.shape, f32)] * 2,
             in_specs=[anywhere] * 2,
-            out_specs=[anywhere] * 2,
+            out_specs=[pl.BlockSpec(memory_space=pltpu.VMEM)] * 2,
             scratch_shapes=[
-                vm(4, 6, planes, nt, lanes),
+                vm(3, 6, planes, nt, lanes),
                 vm(3, 2, 8, 6 * nr, lanes),
                 vm(3, 2, G, 6 * nr, lanes),
                 vm(3, 2, 8, 16, lanes),
@@ -503,10 +520,11 @@
                 vm(9, pad8(long), lanes),
                 vm(6, planes, nt, lanes),
                 vm(4, planes, nt, lanes),
-                vm((nt + 2 * G) * 6 * nr, lanes),
-                vm((nt + 2 * G) * 4 * nr, lanes),
+                vm(pad8((nt + 2 * G) * (6 * nr + PAD)), lanes),
+                vm(pad8((nt + 2 * G) * (4 * nr + PAD)), lanes),
                 vm(6, nr + 1, nt, lanes),
-                vm((nt + 1) * 6 * nr, lanes),
+                vm(pad8((nt + 1) * (6 * nr + PAD)), lanes),
+                vm(9, 2, 8, lanes),
                 vm(6, nr, nt, lanes),
                 vm(planes, 8, lanes),
                 vm(planes, 8, lanes),
@@ -525,6 +543,14 @@
                 collective_id=0, has_side_effects=True
             ),
         )(magnetic, electric)
+        return pl.pallas_call(
+            put_out,
+            out_shape=[jax.ShapeDtypeStruct(magnetic.shape, f32)] * 2,
+            in_specs=[pl.BlockSpec(memory_space=pltpu.VMEM)] * 2,
+            out_specs=[anywhere] * 2,
+            scratch_shapes=[pltpu.SemaphoreType.DMA((2,))],
+            compiler_params=pltpu.CompilerParams(vmem_limit_bytes=4 * 2**20),
+        )(*out)
 
     spec = P(None, "row", "theta", "phi")
     return jax.shard_map(body, mesh=mesh, in_specs=(spec, spec), out_specs=(spec, spec), check_vma=False)

time: 35.5 us -> 26.2 us (0.74)
  Pallas kernels: 32.2 us -> 25.4 us
  local copies, waits for them, and re-layouts: 2.46 us -> 0 us
    pallas_call x1 -> x2, Pallas kernels: 32.2 us -> 25.4 us  [the longest x1 24.6 us: body(): pl.pallas_call(functools.partial(kernel, sizes), out_shape=[pltpu.VMEM(ma...]
    unnamed x4 -> x0, local copies, waits for them, and re-layouts: 2.46 us -> none
where the time goes in v2:
time: 26.2 us; the launch traced here: 26 us
  Pallas kernels  25.4 us (97%)
  between operations  0.64 us (2%)
    pallas_call x1, Pallas kernels, body(): pl.pallas_call(functools.partial(kernel, sizes), out_shape=[pltpu.VMEM(ma...  24.6 us
    pallas_call x1, Pallas kernels, body(): pl.pallas_call(put_out, out_shape=[jax.ShapeDtypeStruct(magnetic.shape, f...  0.83 us

profile of v2, /device:TPU:0, one launch (start us, length us, event | category | flops | bytes accessed | tf_op | source)
XLA Modules:
  0.0 26.0 jit_solution(7937488211641596229)
XLA Ops:
  0.6 24.6 %shard_map.41 = (f32[3,12,16,128]{3,2,1,0:T(8,128)S(1)}, f32[3,12,16,128]{3,2,1,0:T(8,128)S(1)}) custom-call(f32[3,12,16,128]{3,2,1,0:T(8,128)} %mag.1, f32[3,12,16,128]{3,2,1,0:T(8,128)} %ele.1), custom_call_target="tpu_custom_call" | custom-call | tf_op jit(solution)/shard_map/pallas_call | solution.py:508
  25.2 0.8 %shard_map.42 = (f32[3,12,16,128]{3,2,1,0:T(8,128)}, f32[3,12,16,128]{3,2,1,0:T(8,128)}) custom-call(f32[3,12,16,128]{3,2,1,0:T(8,128)S(1)} %get-tuple-element.4.m, f32[3,12,16,128]{3,2,1,0:T(8,128)S(1)} %get-tuple-element.5.e), custom_call_target="tpu_custom_call" | custom-call | tf_op jit(solution)/shard_map/pallas_call | solution.py:546

commit v3 on v2

v3 whole, which is shorter than its diff:
```python
import functools
import math

import jax
import jax.numpy as jnp
from jax import lax
from jax.experimental import pallas as pl
from jax.experimental.pallas import tpu as pltpu
from jax.sharding import PartitionSpec as P

MESH = pl.DeviceIdType.MESH
hole_mass = 1.0
inner_radius = 1.8
wave_speed = 1.25
courant = 0.3
smooth_eps = 1e-06
G = 3

AXES = ((1, 2, 4, 5, 0, 3), (0, 2, 3, 5, 1, 4))
PAD = 1


def kept(make):
    made = {}

    def get(i):
        if i not in made:
            made[i] = make(i)
        return made[i]

    return get


class Line:
    def __init__(self, v):
        self.v = v
        self.d = kept(lambda i: v(i + 1) - v(i))
        self.e = kept(lambda i: self.d(i) * self.d(i) + 4.0 * smooth_eps)
        self.e4 = kept(lambda i: 4.0 * self.e(i))
        self.step = kept(lambda i: self.d(i) - self.d(i - 1))
        self.s2 = kept(lambda i: self.step(i) * self.step(i))
        self.t = kept(lambda i: self.step(i + 1) - self.step(i))
        self.t2 = kept(lambda i: 0.5 * self.t(i))
        self.sum = kept(lambda i: self.e(i - 1) + self.e(i))
        self.rest = kept(lambda i: (11.0 / 3.0) * self.s2(i) - self.sum(i))
        self.mid = kept(lambda i: self.sum(i) + (5.0 / 3.0) * self.s2(i))
        self.low = kept(lambda i: self.rest(i) + self.e4(i))
        self.high = kept(lambda i: self.rest(i) + self.e4(i - 1))
        self.w_low, self.w_mid, self.w_high = (
            kept(lambda i, x=x: self.weight(x(i))) for x in (self.low, self.mid, self.high)
        )
        self.mid6 = kept(lambda i: 6.0 * self.w_mid(i))

    def weight(self, smooth):
        q = pl.reciprocal(smooth, approx=True)
        return q * q

    def up(self, c):
        return ratio(self.low(c - 1), self.mid(c), self.high(c + 1), self.t(c - 1), self.t2(c))

    def down(self, c):
        return ratio(self.high(c + 2), self.mid(c + 1), self.low(c), self.t(c + 1), self.t2(c))

    def both(self, c):
        return blend(
            self.w_low(c - 1), self.mid6(c), 3.0 * self.w_high(c + 1), self.t(c - 1), self.t2(c)
        ) + blend(
            self.w_high(c + 2), self.mid6(c + 1), 3.0 * self.w_low(c), self.t(c + 1), self.t2(c)
        )


def blend(w0, w1, w2, t0, t2):
    den = (w0 + w2) + w1
    return (w0 * t0 + w2 * t2) * pl.reciprocal(den, approx=True)


def ratio(s0, s1, s2, t0, t2):
    y0, y2 = s1 * pl.reciprocal(s0, approx=True), s1 * pl.reciprocal(s2, approx=True)
    return blend(y0 * y0, 6.0, 3.0 * (y2 * y2), t0, t2)


def faces(p, m, f, which):
    line = Line(kept(p))
    if m is None:
        for i in which:
            c = i + 2
            yield i, line.t2(c) - line.both(c)
        return
    other = Line(kept(m))
    f = kept(f)
    f5, f2 = kept(lambda i: 5.0 * f(i)), kept(lambda i: f(i) + f(i))
    for i in which:
        c = i + 2
        lin = (f5(c) + (f2(c + 1) - f(c - 1))) - other.t2(c)
        yield i, lin - (line.up(c) - other.down(c))


def kernel(sizes, mag, ele, mag_out, ele_out, u, ta, tb, ra, rb, pa, pb, qa, qb, tt, dd, vr, vt, gr, gt, ga, acc,
           ca, cs, car, csr, crp, crm, cth, lane_a, lane_s, send, recv, local):
    n_row, n_theta, n_phi, nr, nt, L = sizes
    row, th, ph = lax.axis_index("row"), lax.axis_index("theta"), lax.axis_index("phi")
    halves = nt // 8
    spacing = math.pi / (nt * n_theta)
    spacing_phi = 2.0 * math.pi / (L * n_phi)
    dt = courant / (1.0 / spacing + 1.0 / spacing + 1.0 / spacing_phi)
    scale = -dt / 6.0
    coef_phi = scale / spacing_phi
    planes = nr + 2 * G
    rows6, rows14 = 6 * nr, 14 * nr
    pitch6, pitch14 = rows6 + PAD, rows14 + PAD
    full, rest = L // nt, nr - L // nt
    seg = L // 8
    jump = seg + PAD
    first_row = 16
    sent = ((pa, qa, 0, 6, 24), (pb, qb, 6, 3, 16))
    early = 2 * rest
    groups = ((0, early), (early, rest))
    ta_rows = ta.reshape(3, 2, 8 * 6 * early, L)
    tb_rows = tb.reshape(3, 2, 8 * 6 * rest, L)

    def spot(l, q, late, lines=14):
        return lines * early + l * rest + q - early if late else l * early + q

    def plane_of(q):
        return q + full if isinstance(q, int) and q < rest else (
            q - rest if isinstance(q, int) else jnp.where(q < rest, q + full, q - rest))

    def place(m):
        return m % seg + (m // seg) * jump

    first, last = th == 0, th == n_theta - 1
    opposite = (row, th, lax.rem(ph + n_phi // 2, n_phi))
    right = (row, th, lax.rem(ph + 1, n_phi))
    left = (row, th, lax.rem(ph + n_phi - 1, n_phi))
    above = tuple(jnp.where(last, o, q) for o, q in zip(opposite, (row, th + 1, ph)))
    below = tuple(jnp.where(first, o, q) for o, q in zip(opposite, (row, th - 1, ph)))
    outer, inner = (row + 1, th, ph), (row - 1, th, ph)
    has_outer, has_inner = row < n_row - 1, row > 0

    loads = [
        pltpu.make_async_copy(src, u.at[0, 3 * i : 3 * i + 3, G : G + nr], local.at[i])
        for i, src in enumerate((mag, ele))
    ]
    for c in loads:
        c.start()

    barrier = pltpu.get_barrier_semaphore()
    for target in (above, below, right, left):
        pl.semaphore_signal(barrier, inc=1, device_id=target, device_id_type=MESH)

    @pl.when(has_outer)
    def _():
        pl.semaphore_signal(barrier, inc=1, device_id=outer, device_id_type=MESH)

    @pl.when(has_inner)
    def _():
        pl.semaphore_signal(barrier, inc=1, device_id=inner, device_id_type=MESH)

    lane = lax.broadcasted_iota(jnp.int32, (8, L), 1)
    sub = lax.broadcasted_iota(jnp.int32, (8, L), 0)

    def radius_at(index):
        return inner_radius + (index.astype(jnp.float32) + 0.5) * spacing

    def lapse_shift(radius):
        ratio = 2.0 * hole_mass / radius
        return 1.0 / jnp.sqrt(1.0 + ratio), ratio / (1.0 + ratio)

    for i, (q0, _) in enumerate(groups):
        index = q0 + sub
        a, s = lapse_shift(radius_at(row * nr + jnp.where(index < rest, index + full, index - rest)))
        car[8 * i : 8 * i + 8] = a
        csr[8 * i : 8 * i + 8] = s

    def tables(q, carry):
        index = jnp.full((8, L), row * nr - G + q, jnp.int32)
        a, s = lapse_shift(radius_at(index))
        ca[q] = a
        cs[q] = s
        rc, hi, lo = radius_at(index), radius_at(index + 1), radius_at(index - 1)
        area = scale / (rc * rc * spacing)
        crp[q] = (0.5 * (rc + hi)) ** 2 * area
        crm[q] = (0.5 * (rc + lo)) ** 2 * area
        return carry

    lax.fori_loop(0, planes, tables, 0)
    for q in range(halves):
        index = (th * nt + 8 * q + sub).astype(jnp.float32)
        mid = jnp.sin((index + 0.5) * spacing)
        cth[0, 8 * q : 8 * q + 8] = scale * jnp.sin((index + 1.0) * spacing) / (mid * spacing)
        cth[1, 8 * q : 8 * q + 8] = scale * jnp.sin(index * spacing) / (mid * spacing)

    def owner(x, size):
        out = jnp.zeros((8, L), jnp.int32)
        for q in range(1, L // size):
            out = out + (x >= size * q).astype(jnp.int32)
        return out

    index = owner(lane, nt)
    a, s = lapse_shift(radius_at(row * nr + jnp.where(index < rest, index + full, index - rest)))
    lane_a[0], lane_a[1] = a, -a
    lane_s[0], lane_s[1] = s, s
    second = lane >= L // 2
    a, s = lapse_shift(radius_at(row * nr + rest + owner(jnp.where(second, lane - L // 2, lane), nt)))
    lane_a[2], lane_s[2] = jnp.where(second, -a, a), s

    zeros = jnp.zeros((nt, L), jnp.float32)
    for stage in range(3):
        @pl.when(row == 0)
        def _():
            for c in range(6):
                for q in range(G):
                    u[stage, c, q] = zeros

        @pl.when(row == n_row - 1)
        def _():
            for c in range(6):
                for q in range(G):
                    u[stage, c, G + nr + q] = zeros

    def radial_flux(x, a, s):
        b2, b3, d2, d3 = x[1], x[2], x[4], x[5]
        return [-(a * d3 + s * b2), a * d2 - s * b3, a * b3 - s * d2, -(a * b2 + s * d3)]

    def polar_flux(x, a, s):
        b1, b2, b3, d1, d2, d3 = x
        return [a * d3 + s * b2, -(a * d1), s * d2 - a * b3, a * b1]

    def lines(dim, x, f):
        k = [wave_speed * y for y in x]
        two = [k[c] for c in AXES[dim][:4]]
        return (
            [y + z for y, z in zip(f, two)] + [y - z for y, z in zip(f, two)] + f + [k[c] for c in AXES[dim][4:]]
        )

    def prepare(stage, q, r, tiles, late):
        a, s = ca[r + G], cs[r + G]
        for t in range(halves):
            rows = slice(8 * t, 8 * t + 8)
            x = [tiles[c][t] for c in range(6)]
            for l, y in enumerate(lines(0, x, radial_flux(x, a, s))):
                vr[l, r + G, rows] = y
            for l, y in enumerate(lines(1, x, polar_flux(x, a, s))):
                vt[pl.ds((G + 8 * t) * pitch14 + spot(l, q, late), 8, stride=pitch14), :] = y
            for side, end in enumerate((0, halves - 1)):
                if t == end:
                    for c in range(6):
                        if late:
                            tb_rows[stage, side, pl.ds(c * rest + q - early, 8, stride=6 * rest), :] = x[c]
                        else:
                            ta_rows[stage, side, pl.ds(c * early + q, 8, stride=6 * early), :] = x[c]

    def turn(stage, out, parts):
        x = jnp.concatenate([u[stage, c, G + p : G + p + n].reshape(n * nt, L) for c, p, n in parts], axis=0).T
        for q in range(L // 8):
            tt[out, pl.ds(first_row + place(8 * q), 8), :] = x[8 * q : 8 * q + 8]
        for src, _, b, n, _ in sent:
            if b <= out < b + n:
                src[stage, 0, pl.ds(out - b, 8, stride=n), :] = x[0:8]
                src[stage, 1, pl.ds(out - b, 8, stride=n), :] = x[L - 8 : L]

    def turn_early(stage):
        for c in range(6):
            turn(stage, c, [(c, full, rest), (c, 0, full - rest)])

    def turn_late(stage):
        p = full - rest
        for c in range(3):
            turn(stage, 6 + c, [(c, p, rest), (3 + c, p, rest)])
        for c in range(2):
            turn(stage, 9 + c, [(3 + c, p, rest), (c, p, rest)])

    def remote(src, dst, stage, m_send, m_recv, target):
        return pltpu.make_async_remote_copy(
            src_ref=src, dst_ref=dst, send_sem=send.at[stage, m_send], recv_sem=recv.at[stage, m_recv],
            device_id=target, device_id_type=MESH,
        )

    def radial_out(stage):
        return remote(u.at[stage, :, nr : nr + G], u.at[stage, :, 0:G], stage, 0, 0, outer)

    def radial_in(stage):
        return remote(u.at[stage, :, G : 2 * G], u.at[stage, :, G + nr : nr + 2 * G], stage, 1, 1, inner)

    def theta_copies(stage, late):
        up = jnp.where(last, 1, 0)
        down = jnp.where(first, 0, 1)
        src, dst = (tb, rb) if late else (ta, ra)
        base = 6 if late else 2
        return (
            remote(src.at[stage, 1, 8 - G : 8], dst.at[stage, up], stage, base, base + up, above),
            remote(src.at[stage, 0, 0:G], dst.at[stage, down], stage, base + 1, base + down, below),
        )

    def phi_copies(stage, late):
        src, dst, _, n, edge = sent[late]
        head, tail = pl.ds(0, edge), pl.ds(8 * n - edge, edge)
        base = 8 if late else 4
        return (
            remote(src.at[stage, 1, tail], dst.at[stage, 0, tail], stage, base, base, right),
            remote(src.at[stage, 0, head], dst.at[stage, 1, head], stage, base + 1, base + 1, left),
        )

    def send_early(stage):
        @pl.when(has_outer)
        def _():
            radial_out(stage).start()

        @pl.when(has_inner)
        def _():
            radial_in(stage).start()

        turn_early(stage)
        for c in phi_copies(stage, False) + theta_copies(stage, False):
            c.start()

    def send_late(stage):
        turn_late(stage)
        for c in phi_copies(stage, True) + theta_copies(stage, True):
            c.start()

    for c in loads:
        c.wait()

    def prepare_first(late):
        def part(q, carry):
            r = plane_of(q)
            tiles = [[u[0, c, r + G, 8 * t : 8 * t + 8] for t in range(halves)] for c in range(6)]
            prepare(0, q, r, tiles, late)
            return carry

        return part

    lax.fori_loop(0, early, prepare_first(False), 0)
    lax.fori_loop(early, nr, prepare_first(True), 0)
    pl.semaphore_wait(barrier, 4 + jnp.where(has_outer, 1, 0) + jnp.where(has_inner, 1, 0))
    send_early(0)
    send_late(0)

    def radial_faces(which):
        def part(t, carry):
            rows = pl.ds(pl.multiple_of(8 * t, 8), 8)
            for l in range(6):
                at = lambda j: lambda i: vr[j, i, rows]
                parts = (at(l), at(l + 4), at(l + 8)) if l < 4 else (at(l + 8), None, None)
                for span in which:
                    for i, x in faces(*parts, span):
                        gr[l, i, rows] = x
            return carry

        lax.fori_loop(0, halves, part, 0)

    def polar_faces(lo, hi, which, also):
        def part(q, carry):
            late = lo == 2
            n = rest if late else early
            for j in range(3):
                v = (0 if late else (1 + (j < 2)) * q) + (j if j < 2 else 0)
                base = 14 * early if late else 0
                at = lambda m: lambda i: vt[pl.ds(i * pitch14 + base + 4 * n * m + 8 * v, 8), :]
                parts = (at(0), at(1), at(2)) if j < 2 else (at(3), None, None)
                out = (6 * early if late else 0) + (4 * n if j == 2 else 0) + 8 * v
                for span in which:
                    for i, x in faces(*parts, span):
                        gt[pl.ds(i * pitch6 + out, 8), :] = x
                if also is not None:
                    also(q, j)
            return carry

        lax.fori_loop(lo, hi, part, 0)

    def azimuth_faces(lo, hi, which):
        def part(q, carry):
            a, s = lane_a[q], lane_s[q]
            swapped = jnp.where(q == 0, 3, jnp.where(q == 1, 0, 9))

            def at(block, i):
                return tt[block, pl.ds(first_row + place(i - G), 8, stride=jump), :]

            own = [kept(lambda i, c=c: at(3 * q + c, i)) for c in range(3)]
            fluxes = (
                lambda i: s * own[2](i) - a * at(swapped + 1, i),
                lambda i: a * at(swapped, i),
                None,
            )
            for c in range(3):
                k = kept(lambda i: wave_speed * own[c](i))
                f = kept(fluxes[c]) if fluxes[c] else None
                parts = (lambda i: f(i) + k(i), lambda i: f(i) - k(i), f) if f else (k, None, None)
                for span in which:
                    before = None
                    for i, x in faces(*parts, span):
                        if span[0] == G and (i == G or i == seg - G):
                            ga[3 * q + c, int(i != G)] = x
                        if span[0] == i == seg - G + 1:
                            before = ga[3 * q + c, 1]
                        if before is not None:
                            dd[3 * q + c, pl.ds(i - 1, 8, stride=jump), :] = coef_phi * (x - before)
                        before = x
                    if span == range(0, G):
                        dd[3 * q + c, pl.ds(G - 1, 8, stride=jump), :] = coef_phi * (ga[3 * q + c, 0] - before)
            return carry

        lax.fori_loop(lo, hi, part, 0)

    def turn_back(q, j):
        b = 3 * q + j
        x = jnp.concatenate([dd[b, pl.ds(place(8 * i), 8), :] for i in range(L // 8)], axis=0).T
        acc[b] = x.reshape(full, nt, L)

    inside_r = (range(G, nr - G + 1),)
    edges_r = (range(0, G), range(nr - G + 1, nr + 1))
    inside_t = (range(G, nt - G + 1),)
    inside_a = (range(G, seg - G + 1),)
    edges_a = (range(0, G), range(seg - G + 1, seg + 1))
    edges_t = (range(0, G), range(nt - G + 1, nt + 1))
    whole_t, whole_a = (range(nt + 1),), (range(seg + 1),)

    def azimuth_ghosts(stage, late):
        for c in phi_copies(stage, late):
            c.wait_recv()
        before, after = first_row + place(-G) - (8 - G), first_row + place(L)
        _, dst, b0, n, _ = sent[late]
        for b in range(b0, b0 + n):
            x, y = (dst[stage, i, pl.ds(b - b0, 8, stride=n), :] for i in range(2))
            tt[b, pl.ds(before, 8), :] = x
            tt[b, pl.ds(after, 8), :] = y
            if 6 <= b < 8:
                tt[b + 3, pl.ds(before, 8), :] = pltpu.roll(x, L // 2, 1)
                tt[b + 3, pl.ds(after, 8), :] = pltpu.roll(y, L // 2, 1)

    def polar_ghosts(stage, late):
        src, dst, base = ((ta, ra, 2), (tb, rb, 6))[late]
        q0, n = groups[late]
        a, s = car[8 * late : 8 * late + n], csr[8 * late : 8 * late + n]
        for side in range(2):
            remote(src.at[stage, side, 0:G], dst.at[stage, side], stage, base, base + side, above).wait_recv()
            pole = first if side == 0 else last
            sign = jnp.where(pole, -1.0, 1.0)
            for g in range(G):
                k = jnp.where(pole, G - 1 - g, g)
                target = g if side == 0 else G + nt + g
                x = [dst[stage, side, k, c * n : c * n + n] for c in range(6)]
                x = [y * sign if c % 3 else y for c, y in enumerate(x)]
                for l, y in enumerate(lines(1, x, polar_flux(x, a, s))):
                    vt[pl.ds(target * pitch14 + spot(l, q0, late), n), :] = y

    def stage_body(stage, carry, ending=False):
        radial_faces(inside_r)
        polar_faces(0, 2, inside_t, None)
        azimuth_faces(0, 2, inside_a)

        azimuth_ghosts(stage, 0)
        azimuth_faces(0, 2, edges_a)
        @pl.when(has_inner)
        def _():
            radial_out(stage).wait_recv()

        @pl.when(has_outer)
        def _():
            radial_in(stage).wait_recv()

        def ghost_planes(q, carry):
            p = jnp.where(q < G, q, q + nr)
            a, s = ca[p], cs[p]
            for t in range(halves):
                rows = slice(8 * t, 8 * t + 8)
                x = [u[stage, c, p, rows] for c in range(6)]
                for l, y in enumerate(lines(0, x, radial_flux(x, a, s))):
                    vr[l, p, rows] = y
            return carry

        lax.fori_loop(0, 2 * G, ghost_planes, 0)
        radial_faces(edges_r)

        polar_ghosts(stage, 0)
        polar_faces(0, 2, edges_t, turn_back)

        w = jnp.where(stage == 0, 0.0, jnp.where(stage == 1, 0.75, 1.0 / 3.0)).astype(jnp.float32)

        def update(q, late):
            r = plane_of(q)
            rp, rm = crp[r + G], crm[r + G]
            new = [[None] * halves for _ in range(6)]
            for t in range(halves):
                rows = slice(8 * t, 8 * t + 8)
                for c in range(6):
                    lr, lt = AXES[0].index(c), AXES[1].index(c)
                    at = spot(lt, q, late, 6)
                    low = gt[pl.ds(8 * t * pitch6 + at, 8, stride=pitch6), :]
                    high = gt[pl.ds((8 * t + 1) * pitch6 + at, 8, stride=pitch6), :]
                    block, level = (6 + c % 3, q - early + rest * (c // 3)) if late else (c, q)
                    rate = acc[block, level, rows] + (cth[0, rows] * high - cth[1, rows] * low)
                    rate = rate + (rp * gr[lr, r + 1, rows] - rm * gr[lr, r, rows])
                    new[c][t] = w * u[0, c, r + G, rows] + (1.0 - w) * (u[stage, c, r + G, rows] + rate)
                b, d = [new[c][t] for c in range(3)], [new[c][t] for c in range(3, 6)]
                b2 = jnp.maximum(b[0] * b[0] + b[1] * b[1] + b[2] * b[2], 1.0)
                along = (b[0] * d[0] + b[1] * d[1] + b[2] * d[2]) * pl.reciprocal(b2, approx=True)
                d = [y - along * x for x, y in zip(b, d)]
                d2 = d[0] * d[0] + d[1] * d[1] + d[2] * d[2]
                shrink = b2 * lax.rsqrt(b2 * jnp.maximum(d2, b2))
                for c in range(3):
                    new[3 + c][t] = d[c] * shrink
            return new

        def keep(q, new, late):
            r = plane_of(q)
            for t in range(halves):
                rows = slice(8 * t, 8 * t + 8)
                for c in range(6):
                    if ending:
                        (mag_out, ele_out)[c // 3][c % 3, r, rows] = new[c][t]
                    else:
                        u[stage + 1, c, r + G, rows] = new[c][t]
            if not ending:
                prepare(stage + 1, q, r, new, late)

        def final(late, pair):
            def part(i, carry):
                new = [update(pair * i + j, late) for j in range(pair)]
                for j in range(pair):
                    keep(pair * i + j, new[j], late)
                return carry

            return part

        lax.fori_loop(0, early // 2, final(False, 2), 0)
        if not ending:
            send_early(stage + 1)
        azimuth_ghosts(stage, 1)
        azimuth_faces(2, 3, whole_a)
        polar_ghosts(stage, 1)
        polar_faces(2, 3, whole_t, turn_back)
        lax.fori_loop(early // 2, nr // 2, final(True, 2), 0)
        if not ending:
            send_late(stage + 1)
        return carry

    lax.fori_loop(0, 2, stage_body, 0)
    stage_body(2, 0, True)

    def drain(stage, carry):
        @pl.when(has_outer)
        def _():
            radial_out(stage).wait_send()

        @pl.when(has_inner)
        def _():
            radial_in(stage).wait_send()

        for c in theta_copies(stage, False) + theta_copies(stage, True) + phi_copies(stage, False) + phi_copies(stage, True):
            c.wait_send()
        return carry

    lax.fori_loop(0, 3, drain, 0)


def solution(mesh):
    n_row, n_theta, n_phi = (mesh.shape[k] for k in ("row", "theta", "phi"))

    def put_out(m, e, mo, eo, sem):
        copies = [pltpu.make_async_copy(x, y, sem.at[i]) for i, (x, y) in enumerate(((m, mo), (e, eo)))]
        for c in copies:
            c.start()
        for c in copies:
            c.wait()

    def body(magnetic, electric):
        _, nr, nt, lanes = magnetic.shape
        planes, rest = nr + 2 * G, nr - lanes // nt
        pad8 = lambda n: -(-n // 8) * 8
        f32 = jnp.float32
        vm = lambda *shape: pltpu.VMEM(shape, f32)
        assert nt % 8 == 0 and nr % 4 == 0 and 2 * nr * nt == 3 * lanes
        long = lanes + 8 * PAD
        sizes = (n_row, n_theta, n_phi, nr, nt, lanes)
        anywhere = pl.BlockSpec(memory_space=pl.ANY)
        out = pl.pallas_call(
            functools.partial(kernel, sizes),
            out_shape=[pltpu.VMEM(magnetic.shape, f32)] * 2,
            in_specs=[anywhere] * 2,
            out_specs=[pl.BlockSpec(memory_space=pltpu.VMEM)] * 2,
            scratch_shapes=[
                vm(3, 6, planes, nt, lanes),
                vm(3, 2, 8, 6 * 2 * rest, lanes),
                vm(3, 2, 8, 6 * rest, lanes),
                vm(3, 2, G, 6 * 2 * rest, lanes),
                vm(3, 2, G, 6 * rest, lanes),
                vm(3, 2, 8 * 6, lanes),
                vm(3, 2, 8 * 3, lanes),
                vm(3, 2, 8 * 6, lanes),
                vm(3, 2, 8 * 3, lanes),
                vm(11, 16 + pad8(long) + 8, lanes),
                vm(9, pad8(long), lanes),
                vm(14, planes, nt, lanes),
                vm(pad8((nt + 2 * G) * (14 * nr + PAD)), lanes),
                vm(6, nr + 1, nt, lanes),
                vm(pad8((nt + 1) * (6 * nr + PAD)), lanes),
                vm(9, 2, 8, lanes),
                vm(9, lanes // nt, nt, lanes),
                vm(planes, 8, lanes),
                vm(planes, 8, lanes),
                vm(16, lanes),
                vm(16, lanes),
                vm(planes, 8, lanes),
                vm(planes, 8, lanes),
                vm(2, nt, lanes),
                vm(3, 8, lanes),
                vm(3, 8, lanes),
                pltpu.SemaphoreType.DMA((3, 10)),
                pltpu.SemaphoreType.DMA((3, 10)),
                pltpu.SemaphoreType.DMA((2,)),
            ],
            compiler_params=pltpu.CompilerParams(
                collective_id=0, has_side_effects=True
            ),
        )(magnetic, electric)
        return pl.pallas_call(
            put_out,
            out_shape=[jax.ShapeDtypeStruct(magnetic.shape, f32)] * 2,
            in_specs=[pl.BlockSpec(memory_space=pltpu.VMEM)] * 2,
            out_specs=[anywhere] * 2,
            scratch_shapes=[pltpu.SemaphoreType.DMA((2,))],
            compiler_params=pltpu.CompilerParams(vmem_limit_bytes=4 * 2**20),
        )(*out)

    spec = P(None, "row", "theta", "phi")
    return jax.shard_map(body, mesh=mesh, in_specs=(spec, spec), out_specs=(spec, spec), check_vma=False)
```

time: 26.2 us -> 23.9 us (0.912)
  Pallas kernels: 25.4 us -> 23.1 us
    pallas_call x1, Pallas kernels: 24.6 us -> 22.3 us  [body(): pl.pallas_call(functools.partial(kernel, sizes), out_shape=[pltpu.VMEM(ma...]
where the time goes in v3:
time: 23.9 us; the launch traced here: 23.8 us
  Pallas kernels  23.1 us (97%)
  between operations  0.64 us (3%)
    pallas_call x1, Pallas kernels, body(): pl.pallas_call(functools.partial(kernel, sizes), out_shape=[pltpu.VMEM(ma...  22.3 us
    pallas_call x1, Pallas kernels, body(): pl.pallas_call(put_out, out_shape=[jax.ShapeDtypeStruct(magnetic.shape, f...  0.83 us

profile of v3, /device:TPU:0, one launch (start us, length us, event | category | flops | bytes accessed | tf_op | source)
XLA Modules:
  0.0 23.8 jit_solution(15775192955729501888)
XLA Ops:
  0.6 22.3 %shard_map.41 = (f32[3,12,16,128]{3,2,1,0:T(8,128)S(1)}, f32[3,12,16,128]{3,2,1,0:T(8,128)S(1)}) custom-call(f32[3,12,16,128]{3,2,1,0:T(8,128)} %mag.1, f32[3,12,16,128]{3,2,1,0:T(8,128)} %ele.1), custom_call_target="tpu_custom_call" | custom-call | tf_op jit(solution)/shard_map/pallas_call | solution.py:578
  22.9 0.8 %shard_map.42 = (f32[3,12,16,128]{3,2,1,0:T(8,128)}, f32[3,12,16,128]{3,2,1,0:T(8,128)}) custom-call(f32[3,12,16,128]{3,2,1,0:T(8,128)S(1)} %get-tuple-element.4.m, f32[3,12,16,128]{3,2,1,0:T(8,128)S(1)} %get-tuple-element.5.e), custom_call_target="tpu_custom_call" | custom-call | tf_op jit(solution)/shard_map/pallas_call | solution.py:618

commit v4 on v3

--- a/solution.py
+++ b/solution.py
@@ -310,7 +310,8 @@
         def _():
             radial_in(stage).start()
 
-        turn_early(stage)
+        if not (isinstance(stage, int) and stage == 0):
+            turn_early(stage)
         for c in phi_copies(stage, False) + theta_copies(stage, False):
             c.start()
 
@@ -333,6 +334,7 @@
 
     lax.fori_loop(0, early, prepare_first(False), 0)
     lax.fori_loop(early, nr, prepare_first(True), 0)
+    turn_early(0)
     pl.semaphore_wait(barrier, 4 + jnp.where(has_outer, 1, 0) + jnp.where(has_inner, 1, 0))
     send_early(0)
     send_late(0)
@@ -414,7 +416,6 @@
     inside_a = (range(G, seg - G + 1),)
     edges_a = (range(0, G), range(seg - G + 1, seg + 1))
     edges_t = (range(0, G), range(nt - G + 1, nt + 1))
-    whole_t, whole_a = (range(nt + 1),), (range(seg + 1),)
 
     def azimuth_ghosts(stage, late):
         for c in phi_copies(stage, late):
@@ -448,7 +449,8 @@
     def stage_body(stage, carry, ending=False):
         radial_faces(inside_r)
         polar_faces(0, 2, inside_t, None)
-        azimuth_faces(0, 2, inside_a)
+        azimuth_faces(0, 3, inside_a)
+        polar_faces(2, 3, inside_t, None)
 
         azimuth_ghosts(stage, 0)
         azimuth_faces(0, 2, edges_a)
@@ -528,9 +530,9 @@
         if not ending:
             send_early(stage + 1)
         azimuth_ghosts(stage, 1)
-        azimuth_faces(2, 3, whole_a)
+        azimuth_faces(2, 3, edges_a)
         polar_ghosts(stage, 1)
-        polar_faces(2, 3, whole_t, turn_back)
+        polar_faces(2, 3, edges_t, turn_back)
         lax.fori_loop(early // 2, nr // 2, final(True, 2), 0)
         if not ending:
             send_late(stage + 1)

time: 23.9 us -> 23.3 us (0.975)
  Pallas kernels: 23.1 us -> 22.4 us
    pallas_call x1, Pallas kernels: 22.3 us -> 21.6 us  [body(): pl.pallas_call(functools.partial(kernel, sizes), out_shape=[pltpu.VMEM(ma...]
where the time goes in v4:
time: 23.3 us; the launch traced here: 23 us
  Pallas kernels  22.4 us (96%)
  between operations  0.64 us (3%)
    pallas_call x1, Pallas kernels, body(): pl.pallas_call(functools.partial(kernel, sizes), out_shape=[pltpu.VMEM(ma...  21.6 us
    pallas_call x1, Pallas kernels, body(): pl.pallas_call(put_out, out_shape=[jax.ShapeDtypeStruct(magnetic.shape, f...  0.83 us

profile of v4, /device:TPU:0, one launch (start us, length us, event | category | flops | bytes accessed | tf_op | source)
XLA Modules:
  0.0 23.0 jit_solution(8343200532722662359)
XLA Ops:
  0.6 21.6 %shard_map.41 = (f32[3,12,16,128]{3,2,1,0:T(8,128)S(1)}, f32[3,12,16,128]{3,2,1,0:T(8,128)S(1)}) custom-call(f32[3,12,16,128]{3,2,1,0:T(8,128)} %mag.1, f32[3,12,16,128]{3,2,1,0:T(8,128)} %ele.1), custom_call_target="tpu_custom_call" | custom-call | tf_op jit(solution)/shard_map/pallas_call | solution.py:580
  22.2 0.8 %shard_map.42 = (f32[3,12,16,128]{3,2,1,0:T(8,128)}, f32[3,12,16,128]{3,2,1,0:T(8,128)}) custom-call(f32[3,12,16,128]{3,2,1,0:T(8,128)S(1)} %get-tuple-element.4.m, f32[3,12,16,128]{3,2,1,0:T(8,128)S(1)} %get-tuple-element.5.e), custom_call_target="tpu_custom_call" | custom-call | tf_op jit(solution)/shard_map/pallas_call | solution.py:620

commit v5 on v4

--- a/solution.py
+++ b/solution.py
@@ -137,24 +137,24 @@
     outer, inner = (row + 1, th, ph), (row - 1, th, ph)
     has_outer, has_inner = row < n_row - 1, row > 0
 
+    barrier = pltpu.get_barrier_semaphore()
+    for target in (above, below, right, left):
+        pl.semaphore_signal(barrier, inc=1, device_id=target, device_id_type=MESH)
+
+    @pl.when(has_outer)
+    def _():
+        pl.semaphore_signal(barrier, inc=1, device_id=outer, device_id_type=MESH)
+
+    @pl.when(has_inner)
+    def _():
+        pl.semaphore_signal(barrier, inc=1, device_id=inner, device_id_type=MESH)
+
     loads = [
         pltpu.make_async_copy(src, u.at[0, 3 * i : 3 * i + 3, G : G + nr], local.at[i])
         for i, src in enumerate((mag, ele))
     ]
     for c in loads:
         c.start()
-
-    barrier = pltpu.get_barrier_semaphore()
-    for target in (above, below, right, left):
-        pl.semaphore_signal(barrier, inc=1, device_id=target, device_id_type=MESH)
-
-    @pl.when(has_outer)
-    def _():
-        pl.semaphore_signal(barrier, inc=1, device_id=outer, device_id_type=MESH)
-
-    @pl.when(has_inner)
-    def _():
-        pl.semaphore_signal(barrier, inc=1, device_id=inner, device_id_type=MESH)
 
     lane = lax.broadcasted_iota(jnp.int32, (8, L), 1)
     sub = lax.broadcasted_iota(jnp.int32, (8, L), 0)

time: 23.3 us -> 23.3 us (level)
  no operation moved by 1% of the time
where the time goes in v5:
time: 23.3 us; the launch traced here: 23 us
  Pallas kernels  22.4 us (96%)
  between operations  0.64 us (3%)
    pallas_call x1, Pallas kernels, body(): pl.pallas_call(functools.partial(kernel, sizes), out_shape=[pltpu.VMEM(ma...  21.5 us
    pallas_call x1, Pallas kernels, body(): pl.pallas_call(put_out, out_shape=[jax.ShapeDtypeStruct(magnetic.shape, f...  0.83 us

profile of v5, /device:TPU:0, one launch (start us, length us, event | category | flops | bytes accessed | tf_op | source)
XLA Modules:
  0.0 23.0 jit_solution(11233880973747425355)
XLA Ops:
  0.6 21.5 %shard_map.41 = (f32[3,12,16,128]{3,2,1,0:T(8,128)S(1)}, f32[3,12,16,128]{3,2,1,0:T(8,128)S(1)}) custom-call(f32[3,12,16,128]{3,2,1,0:T(8,128)} %mag.1, f32[3,12,16,128]{3,2,1,0:T(8,128)} %ele.1), custom_call_target="tpu_custom_call" | custom-call | tf_op jit(solution)/shard_map/pallas_call | solution.py:580
  22.2 0.8 %shard_map.42 = (f32[3,12,16,128]{3,2,1,0:T(8,128)}, f32[3,12,16,128]{3,2,1,0:T(8,128)}) custom-call(f32[3,12,16,128]{3,2,1,0:T(8,128)S(1)} %get-tuple-element.4.m, f32[3,12,16,128]{3,2,1,0:T(8,128)S(1)} %get-tuple-element.5.e), custom_call_target="tpu_custom_call" | custom-call | tf_op jit(solution)/shard_map/pallas_call | solution.py:620
